TPU v7x, 32 devices: a whole 2x2x4 slice. The times are simulated.
32 devices in a mesh: groups: 2 (over y), frame: 4 (over z), space: 2 (over x), head: 2 (over core).
Axes of the slice: x: 2, y: 2, z: 4, core: 2. Of those that a mesh axis runs over, the one named last changes fastest.
Arguments:
- queries: bfloat16 [8, 512, 3072], P(('groups', 'frame'), 'space', 'head'), parts along dimension 0, may hold values from -6 to 6
- key_states: bfloat16 [8, 512, 3072], P(('groups', 'frame'), 'space', 'head'), parts along dimension 0, may hold values from -24 to 24
- value_states: bfloat16 [8, 512, 3072], P(('groups', 'frame'), 'space', 'head'), parts along dimension 0, may hold values from -6 to 6
- profile: int32 [24], replicated, may hold values from 0 to 1, as said below
- window: int32 [24], replicated, may hold values from 1 to 4, as said below
Outputs:
- attended: bfloat16 [8, 512, 3072], P(('groups', 'frame'), 'space', 'head'), parts along dimension 0
There are 2 independent parts, one for each index of `groups`. A program takes and returns all parts, laid end to end along the dimension named above; an argument that names none is the same for every part. Nothing has to cross between parts.
Inputs may be any that keep to these rules, and one draw needn't show every extreme that they name: `profile`: 1 marks a head of frame-local attention, 0 a head of attention over a window of frames; exactly half of the 24 heads are marked 1. Some head marked 0 in profile has window 4.
All inputs are finite; a program needn't handle non-finite values.
Results may differ from a plain program's by a relative error of at most 0.0055.
Values may be sent and summed in bfloat16 or wider, within the bound.
A program may use at most 64 MiB of HBM per device.

v0:
```python
import jax
import jax.numpy as jnp
from jax import lax
from jax.sharding import PartitionSpec as P

H = 24
HD = 128
WMAX = 4


def from_behind(block, axis, distance):
    devices = range(lax.axis_size(axis))
    route = [(i - distance, i) for i in devices if i - distance in devices]
    return lax.ppermute(block, axis, route)


def spatial(query_rows, key_rows, value_rows):
    row_count, head_count = (query_rows.shape[0], query_rows.shape[1])
    scale = HD ** (-0.5)
    query_major = jnp.moveaxis(query_rows, 1, 0)
    start_state = (
        jnp.full((head_count, row_count), -1e30, jnp.float32),
        jnp.zeros((head_count, row_count), jnp.float32),
        jnp.zeros((head_count, row_count, HD), jnp.float32),
    )
    key_major = jnp.moveaxis(lax.all_gather(key_rows, "space", axis=0, tiled=True), 1, 0)
    value_major = jnp.moveaxis(lax.all_gather(value_rows, "space", axis=0, tiled=True), 1, 0)

    def one_head(item):
        query_one, key_one, value_one, running_max, running_sum, accum = item
        scores = jnp.dot(query_one, key_one.T, preferred_element_type=jnp.float32) * scale
        new_max = jnp.maximum(running_max, jnp.max(scores, axis=1))
        factor = jnp.exp(running_max - new_max)
        weights = jnp.exp(scores - new_max[:, None])
        new_sum = running_sum * factor + jnp.sum(weights, axis=1)
        product = jnp.dot(
            weights.astype(jnp.bfloat16), value_one, preferred_element_type=jnp.float32
        )
        return (new_max, new_sum, accum * factor[:, None] + product)

    final_max, final_sum, final_accum = lax.map(
        one_head, (query_major, key_major, value_major) + tuple(start_state)
    )
    return jnp.moveaxis(final_accum / final_sum[:, :, None], 0, 1)


def temporal(query_rows, key_rows, value_rows, reach_frames):
    scale = HD ** (-0.5)
    frame_index = lax.axis_index("frame")
    frame_total = lax.axis_size("frame")
    score_list = []
    value_list = []
    for offset in range(-WMAX, WMAX + 1):
        if offset == 0:
            near_keys, near_values = (key_rows, value_rows)
        else:
            near_keys, near_values = from_behind((key_rows, value_rows), "frame", -offset)
        raw_scores = (
            jnp.einsum("rhd,rhd->rh", query_rows, near_keys, preferred_element_type=jnp.float32)
            * scale
        )
        in_range = (frame_index + offset >= 0) & (frame_index + offset < frame_total)
        inside = in_range & (reach_frames >= abs(offset))
        score_list.append(jnp.where(inside[None, :], raw_scores, -1e30))
        value_list.append(near_values)
    scores = jnp.stack(score_list)
    peak = jnp.max(scores, axis=0)
    weights = jnp.exp(scores - peak[None])
    denominator = jnp.sum(weights, axis=0)
    numerator = jnp.einsum(
        "orh,orhd->rhd",
        weights.astype(jnp.bfloat16),
        jnp.stack(value_list),
        preferred_element_type=jnp.float32,
    )
    return numerator / denominator[:, :, None]


def local(queries, key_states, value_states, profile, window):
    head_here = queries.shape[2] // HD
    row_count = queries.shape[0] * queries.shape[1]
    core_index = lax.axis_index("head")
    whole_query, whole_key, whole_value = (
        lax.all_gather(queries, "head", axis=2, tiled=True),
        lax.all_gather(key_states, "head", axis=2, tiled=True),
        lax.all_gather(value_states, "head", axis=2, tiled=True),
    )
    core_count = lax.axis_size("head")
    share = H // 2 // core_count
    spatial_order = jnp.argsort(1 - profile, stable=True)
    window_order = jnp.argsort(profile, stable=True)
    mine_spatial = lax.dynamic_slice_in_dim(spatial_order, core_index * share, share)
    mine_window = lax.dynamic_slice_in_dim(window_order, core_index * share, share)
    query_all = whole_query.reshape(row_count, H, HD)
    key_all = whole_key.reshape(row_count, H, HD)
    value_all = whole_value.reshape(row_count, H, HD)
    spatial_part = spatial(
        jnp.take(query_all, mine_spatial, axis=1),
        jnp.take(key_all, mine_spatial, axis=1),
        jnp.take(value_all, mine_spatial, axis=1),
    ).astype(jnp.bfloat16)
    window_query = jnp.take(query_all, mine_window, axis=1)
    window_key = jnp.take(key_all, mine_window, axis=1)
    window_value = jnp.take(value_all, mine_window, axis=1)
    window_reach = jnp.take(window, mine_window)
    window_part = temporal(window_query, window_key, window_value, window_reach).astype(
        jnp.bfloat16
    )
    finished = jnp.concatenate([spatial_part, window_part], axis=1)
    finished = finished.reshape(queries.shape[0], queries.shape[1], 2 * share * HD)
    every_result = lax.all_gather(finished, "head", axis=2, tiled=True)
    half_count = H // 2
    all_ids = jnp.concatenate(
        [
            spatial_order[:half_count].reshape(core_count, share),
            window_order[:half_count].reshape(core_count, share),
        ],
        axis=1,
    ).reshape(-1)
    wanted = core_index * head_here + jnp.arange(head_here, dtype=jnp.int32)
    selector = (all_ids[None, :] == wanted[:, None]).astype(jnp.bfloat16)
    every_heads = every_result.reshape(queries.shape[0], queries.shape[1], H, HD)
    picked = jnp.einsum("jh,frhd->frjd", selector, every_heads, preferred_element_type=jnp.float32)
    return picked.astype(jnp.bfloat16).reshape(queries.shape)


def solution(mesh):
    placed = (
        P(("groups", "frame"), "space", "head"),
        P(("groups", "frame"), "space", "head"),
        P(("groups", "frame"), "space", "head"),
        P(),
        P(),
    )
    return jax.shard_map(
        local,
        mesh=mesh,
        in_specs=placed,
        out_specs=P(("groups", "frame"), "space", "head"),
        check_vma=False,
    )
```

profile of v0, /device:TPU:0, one launch (start us, length us, event | category | flops | bytes accessed | tf_op | source)
XLA Modules:
  0.0 171.8 jit_solution(14820227157894877132)
XLA Ops:
  6.5 2.4 %copy.25 = bf16[1,256,1536]{1,2,0:T(8,128)(2,1)} copy(bf16[1,256,1536]{2,1,0:T(8,128)(2,1)} %param.10) | data formatting | bytes 1572864 | tf_op args[1]
  9.0 2.3 %copy.27 = bf16[1,256,1536]{1,2,0:T(8,128)(2,1)} copy(bf16[1,256,1536]{2,1,0:T(8,128)(2,1)} %param.11) | data formatting | bytes 1572864 | tf_op args[2]
  11.3 1.2 copy.23
  12.7 1.7 sort.32
  14.4 1.7 sort.31
  18.5 3.1 %all-gather.7.cloned.1.call-done = bf16[1,256,3072]{1,2,0:T(8,128)(2,1)} async-done(((bf16[1,256,1536]{1,2,0:T(8,128)(2,1)}), bf16[1,256,3072]{1,2,0:T(8,128)(2,1)}) %all-gather.7.cloned.1.call-update) | async-done | bytes 1572880 | tf_op jit(solution)/shard_map/all_gather | solution.py:85
  21.6 1.9 %copy.26 = bf16[256,24,128]{2,0,1:T(8,128)(2,1)S(1)} copy(bf16[256,24,128]{0,2,1:T(8,128)(2,1)} %bitcast.112) | data formatting | bytes 3145728 | tf_op jit(solution)/shard_map/reshape | solution.py:95
  24.8 9.7 %all-gather.9.cloned.1.call-done = bf16[1,256,3072]{1,2,0:T(8,128)(2,1)} async-done(((bf16[1,256,1536]{1,2,0:T(8,128)(2,1)}), bf16[1,256,3072]{1,2,0:T(8,128)(2,1)}) %all-gather.9.cloned.1.call-update) | async-done | bytes 1572880 | tf_op jit(solution)/shard_map/all_gather | solution.py:86
  34.5 1.9 %copy.28 = bf16[256,24,128]{2,0,1:T(8,128)(2,1)S(1)} copy(bf16[256,24,128]{0,2,1:T(8,128)(2,1)} %bitcast.113) | data formatting | bytes 3145728 | tf_op jit(solution)/shard_map/reshape | solution.py:96
  37.7 1.5 fusion.24
  39.2 1.3 collective-permute-start.6
  40.5 1.3 collective-permute-start.5
  41.8 1.3 collective-permute-start.4
  43.1 5.3 %collective-permute-start.3 = (bf16[256,6,128]{2,0,1:T(8,128)(2,1)S(1)}, bf16[256,6,128]{2,0,1:T(8,128)(2,1)}, u32[]{:S(2)}, u32[]{:S(2)}) collective-permute-start(bf16[256,6,128]{2,0,1:T(8,128)(2,1)S(1)} %get-tuple-element.81), channel_id=1, source_target_pairs={{0,4},{4,8},{8,12},{1,5},{5,9},{9,13},{2,6},{6,10},{10,14},{3,7},{... | collective-permute-start | bytes 1179656 | tf_op jit(solution)/shard_map/ppermute | solution.py:14
  48.4 7.0 %collective-permute-start.2 = (bf16[256,6,128]{2,0,1:T(8,128)(2,1)S(1)}, bf16[256,6,128]{2,0,1:T(8,128)(2,1)}, u32[]{:S(2)}, u32[]{:S(2)}) collective-permute-start(bf16[256,6,128]{2,0,1:T(8,128)(2,1)S(1)} %get-tuple-element.81), channel_id=1, source_target_pairs={{0,8},{4,12},{1,9},{5,13},{2,10},{6,14},{3,11},{7,15},{16,24},{20,... | collective-permute-start | bytes 1179656 | tf_op jit(solution)/shard_map/ppermute | solution.py:14
  55.4 1.9 %copy.24 = bf16[256,24,128]{2,0,1:T(8,128)(2,1)S(1)} copy(bf16[256,24,128]{0,2,1:T(8,128)(2,1)} %bitcast.111) | data formatting | bytes 3145728 | tf_op jit(solution)/shard_map/reshape | solution.py:94
  57.3 0.7 gather_fusion.1
  58.1 1.6 select_bitcast_fusion.1
  59.6 10.8 %all_gather.22 = bf16[512,6,128]{2,0,1:T(8,128)(2,1)S(1)} all-gather(bf16[256,6,128]{2,0,1:T(8,128)(2,1)S(1)} %get-tuple-element.77), channel_id=1, replica_groups=mesh['groups'=2,'frame'=4,'space'=2,'head'=2] {'space'}, dimensions={0}, use_global_device_ids=true | all-gather | bytes 1179648 | tf_op jit(solution)/shard_map/all_gather | solution.py:27
  70.5 10.2 %all_gather.20 = bf16[512,6,128]{2,0,1:T(8,128)(2,1)} all-gather(bf16[256,6,128]{2,0,1:T(8,128)(2,1)S(1)} %get-tuple-element.78), channel_id=1, replica_groups=mesh['groups'=2,'frame'=4,'space'=2,'head'=2] {'space'}, dimensions={0}, use_global_device_ids=true | all-gather | bytes 1179648 | tf_op jit(solution)/shard_map/all_gather | solution.py:26
  80.7 2.0 %collective-permute-start.1 = (bf16[256,6,128]{2,0,1:T(8,128)(2,1)S(1)}, bf16[256,6,128]{2,0,1:T(8,128)(2,1)}, u32[]{:S(2)}, u32[]{:S(2)}) collective-permute-start(bf16[256,6,128]{2,0,1:T(8,128)(2,1)S(1)} %get-tuple-element.81), channel_id=1, source_target_pairs={{0,12},{1,13},{2,14},{3,15},{16,28},{17,29},{18,30},{19,31}} | collective-permute-start | bytes 1179656 | tf_op jit(solution)/shard_map/ppermute | solution.py:14
  82.7 1.4 collective-permute-start
  84.1 15.7 %while.12 = (s32[]{:T(128)}, f32[6,256]{1,0:T(8,128)S(1)}, f32[6,256,128]{1,2,0:T(8,128)}, bf16[6,256,128]{2,1,0:T(8,128)(2,1)}, bf16[6,512,128]{2,1,0:T(8,128)(...) while((s32[]{:T(128)}, f32[6,256]{1,0:T(8,128)S(1)}, f32[6,256,128]{1,2,0:T(8,128)}, ...), condition=%wide.region_4.6_spmd, body=%wide.region_1.5_spmd.sunk | while | flops 67928832 | bytes 2570345 | solution.py:41
  84.1 1.2 fusion.42
  86.7 1.3 fusion.42
  89.3 1.2 fusion.42
  91.3 0.7 constant_dynamic-update-slice_fusion.11
  92.0 1.2 fusion.42
  93.9 0.7 constant_dynamic-update-slice_fusion.11
  94.6 1.3 fusion.42
  97.2 1.3 fusion.42
  100.5 1.2 fusion.23
  101.8 1.3 collective-permute-start.12
  103.1 1.3 collective-permute-start.11
  104.4 1.3 collective-permute-start.13
  105.7 7.6 %collective-permute-start.8 = (bf16[256,6,128]{2,0,1:T(8,128)(2,1)}, bf16[256,6,128]{2,0,1:T(8,128)(2,1)S(1)}, u32[]{:S(2)}, u32[]{:S(2)}) collective-permute-start(bf16[256,6,128]{2,0,1:T(8,128)(2,1)} %get-tuple-element.80), channel_id=1, source_target_pairs={{0,12},{1,13},{2,14},{3,15},{16,28},{17,29},{18,30},{19,31}} | collective-permute-start | bytes 1179656 | tf_op jit(solution)/shard_map/ppermute | solution.py:14
  113.4 0.7 collective-permute-start.7
  114.1 3.5 %fusion.22 = (f32[256,6]{0,1:T(8,128)S(1)}, f32[256,6]{0,1:T(8,128)S(1)}, f32[256,6]{0,1:T(8,128)S(1)}, f32[256,6]{0,1:T(8,128)S(1)}, f32[256,6]{0,1:T(8,128)S(1...) fusion(bf16[256,6,128]{2,0,1:T(8,128)(2,1)} %collective-permute-done.6, ...), kind=kLoop, calls=%fused_computation.44 | loop fusion | flops 5099520 | bytes 3588102 | tf_op jit(solution)/shard_map/rhd,rhd->rh/dot_general | solution.py:59
  118.1 1.3 collective-permute-start.10
  119.4 2.4 %collective-permute-done.8 = bf16[256,6,128]{2,0,1:T(8,128)(2,1)S(1)} collective-permute-done((bf16[256,6,128]{2,0,1:T(8,128)(2,1)}, bf16[256,6,128]{2,0,1:T(8,128)(2,1)S(1)}, u32[]{:S(2)}, u32[]{:S(2)}) %collective-permute-start.8) | collective-permute-done | bytes 393248 | tf_op jit(solution)/shard_map/ppermute | solution.py:14
  121.8 1.3 collective-permute-start.9
  123.4 12.6 %collective-permute-done.9 = bf16[256,6,128]{2,0,1:T(8,128)(2,1)S(1)} collective-permute-done((bf16[256,6,128]{2,0,1:T(8,128)(2,1)S(1)}, bf16[256,6,128]{2,0,1:T(8,128)(2,1)S(1)}, u32[]{:S(2)}, u32[]{:S(2)}) %collective-permute-start.9) | collective-permute-done | bytes 393248 | tf_op jit(solution)/shard_map/ppermute | solution.py:14
  136.8 2.2 %multiply_reduce_fusion = f32[256,6,128]{2,0,1:T(8,128)S(1)} fusion(f32[256,6,9]{0,1,2:T(8,128)S(1)} %get-tuple-element.76, bf16[9,256,6,128]{3,1,2,0:T(8,128)(2,1)S(1)} %bitcast_dynamic-update-slice_fusion.8), kind=kLoop, calls=%fused_computation.26 | loop fusion | flops 5111808 | bytes 4380672
  139.3 0.9 pad_maximum_fusion
  140.7 20.0 %all-gather.11.cloned.1.call-done = bf16[1,256,3072]{1,2,0:T(8,128)(2,1)} async-done(((bf16[1,256,1536]{1,2,0:T(8,128)(2,1)}), bf16[1,256,3072]{1,2,0:T(8,128)(2,1)}) %all-gather.11.cloned.1.call-update) | async-done | bytes 1572880 | tf_op jit(solution)/shard_map/all_gather | solution.py:111
  160.7 2.0 %copy.83 = bf16[256,24,128]{2,1,0:T(8,128)(2,1)S(1)} copy(bf16[256,24,128]{0,2,1:T(8,128)(2,1)} %bitcast.114) | data formatting | bytes 3145728 | tf_op jit(solution)/shard_map/reshape.2
  163.2 0.9 copy.34
  164.1 1.2 copy.35
  (143 shorter events, 15.0 us)
Async XLA Ops:
  6.5 10.2 %copy-start = (s32[24]{0:T(128)S(1)}, s32[24]{0:T(128)}, u32[]{:S(2)}) copy-start(s32[24]{0:T(128)} %param.13) | copy-start | bytes 292
  6.5 4.8 %copy-start.1 = (bf16[1,256,1536]{2,1,0:T(8,128)(2,1)S(1)}, bf16[1,256,1536]{2,1,0:T(8,128)(2,1)}, u32[]{:S(2)}) copy-start(bf16[1,256,1536]{2,1,0:T(8,128)(2,1)} %param.9) | copy-start | bytes 2359300
  6.5 6.1 %copy-start.18 = (s32[24]{0:T(128)S(1)}, s32[24]{0:T(128)}, u32[]{:S(2)}) copy-start(s32[24]{0:T(128)} %param.12) | copy-start | bytes 292
  6.5 15.1 %all-gather.7.cloned.1.call-start = ((), (), s32[]{:S(2)}) async-start(), calls=%async_computation.1 | async-start | bytes 2359296 | tf_op jit(solution)/shard_map/all_gather | solution.py:85
  8.9 25.5 %all-gather.9.cloned.1.call-start = ((), (), s32[]{:S(2)}) async-start(), calls=%async_computation.2 | async-start | bytes 2359296 | tf_op jit(solution)/shard_map/all_gather | solution.py:86
  11.3 44.1 %all-gather.5.cloned.1.call-start = ((), (), s32[]{:S(2)}) async-start(), calls=%async_computation | async-start | bytes 2359296 | tf_op jit(solution)/shard_map/all_gather | solution.py:84
  12.5 148.2 %all-gather.11.cloned.1.call-start = ((), (), s32[]{:S(2)}) async-start(), calls=%async_computation.3 | async-start | bytes 2359296 | tf_op jit(solution)/shard_map/all_gather | solution.py:111
  14.4 2.4 %copy-start.14 = (s32[24]{0:T(128)}, s32[24]{0:T(128)S(1)}, u32[]{:S(2)}) copy-start(s32[24]{0:T(128)S(1)} %get-tuple-element.44) | copy-start | bytes 292
  16.1 20.3 %copy-start.16 = (s32[24]{0:T(128)}, s32[24]{0:T(128)S(1)}, u32[]{:S(2)}) copy-start(s32[24]{0:T(128)S(1)} %get-tuple-element.41) | copy-start | bytes 292
  17.4 19.6 %copy-start.4 = (s32[1024]{0:T(1024)}, s32[1024]{0:T(1024)S(1)}, u32[]{:S(2)}) copy-start(s32[1024]{0:T(1024)S(1)} %pad_clamp_fusion.1) | copy-start | bytes 12292
  39.2 41.5 %collective-permute-start.6 = (bf16[256,6,128]{2,0,1:T(8,128)(2,1)S(1)}, bf16[256,6,128]{2,0,1:T(8,128)(2,1)}, u32[]{:S(2)}, u32[]{:S(2)}) collective-permute-start(bf16[256,6,128]{2,0,1:T(8,128)(2,1)S(1)} %get-tuple-element.81), channel_id=1, source_target_pairs={{12,0},{13,1},{14,2},{15,3},{28,16},{29,17},{30,18},{31,19}} | collective-permute-start | bytes 1179656 | tf_op jit(solution)/shard_map/ppermute | solution.py:14
  40.5 42.2 %collective-permute-start.5 = (bf16[256,6,128]{2,0,1:T(8,128)(2,1)S(1)}, bf16[256,6,128]{2,0,1:T(8,128)(2,1)}, u32[]{:S(2)}, u32[]{:S(2)}) collective-permute-start(bf16[256,6,128]{2,0,1:T(8,128)(2,1)S(1)} %get-tuple-element.81), channel_id=1, source_target_pairs={{8,0},{12,4},{9,1},{13,5},{10,2},{14,6},{11,3},{15,7},{24,16},{28,... | collective-permute-start | bytes 1179656 | tf_op jit(solution)/shard_map/ppermute | solution.py:14
  41.8 60.0 %collective-permute-start.4 = (bf16[256,6,128]{2,0,1:T(8,128)(2,1)S(1)}, bf16[256,6,128]{2,0,1:T(8,128)(2,1)}, u32[]{:S(2)}, u32[]{:S(2)}) collective-permute-start(bf16[256,6,128]{2,0,1:T(8,128)(2,1)S(1)} %get-tuple-element.81), channel_id=1, source_target_pairs={{4,0},{8,4},{12,8},{5,1},{9,5},{13,9},{6,2},{10,6},{14,10},{7,3},{... | collective-permute-start | bytes 1179656 | tf_op jit(solution)/shard_map/ppermute | solution.py:14
  43.1 60.0 %collective-permute-start.3 = (bf16[256,6,128]{2,0,1:T(8,128)(2,1)S(1)}, bf16[256,6,128]{2,0,1:T(8,128)(2,1)}, u32[]{:S(2)}, u32[]{:S(2)}) collective-permute-start(bf16[256,6,128]{2,0,1:T(8,128)(2,1)S(1)} %get-tuple-element.81), channel_id=1, source_target_pairs={{0,4},{4,8},{8,12},{1,5},{5,9},{9,13},{2,6},{6,10},{10,14},{3,7},{... | collective-permute-start | bytes 1179656 | tf_op jit(solution)/shard_map/ppermute | solution.py:14
  48.4 56.0 %collective-permute-start.2 = (bf16[256,6,128]{2,0,1:T(8,128)(2,1)S(1)}, bf16[256,6,128]{2,0,1:T(8,128)(2,1)}, u32[]{:S(2)}, u32[]{:S(2)}) collective-permute-start(bf16[256,6,128]{2,0,1:T(8,128)(2,1)S(1)} %get-tuple-element.81), channel_id=1, source_target_pairs={{0,8},{4,12},{1,9},{5,13},{2,10},{6,14},{3,11},{7,15},{16,24},{20,... | collective-permute-start | bytes 1179656 | tf_op jit(solution)/shard_map/ppermute | solution.py:14
  80.7 25.1 %collective-permute-start.1 = (bf16[256,6,128]{2,0,1:T(8,128)(2,1)S(1)}, bf16[256,6,128]{2,0,1:T(8,128)(2,1)}, u32[]{:S(2)}, u32[]{:S(2)}) collective-permute-start(bf16[256,6,128]{2,0,1:T(8,128)(2,1)S(1)} %get-tuple-element.81), channel_id=1, source_target_pairs={{0,12},{1,13},{2,14},{3,15},{16,28},{17,29},{18,30},{19,31}} | collective-permute-start | bytes 1179656 | tf_op jit(solution)/shard_map/ppermute | solution.py:14
  82.7 30.7 %collective-permute-start = (bf16[256,6,128]{2,0,1:T(8,128)(2,1)S(1)}, bf16[256,6,128]{2,0,1:T(8,128)(2,1)}, u32[]{:S(2)}, u32[]{:S(2)}) collective-permute-start(bf16[256,6,128]{2,0,1:T(8,128)(2,1)S(1)} %get-tuple-element.81), channel_id=1, source_target_pairs={} | collective-permute-start | bytes 1179656 | tf_op jit(solution)/shard_map/ppermute | solution.py:14
  100.4 17.1 %copy-start.13 = (pred[6]{0:T(512)(128)(4,1)S(1)}, pred[6]{0:T(512)(128)(4,1)}, u32[]{:S(2)}) copy-start(pred[6]{0:T(512)(128)(4,1)} %get-tuple-element.89) | copy-start | bytes 22
  100.4 17.2 %copy-start.12 = (pred[6]{0:T(512)(128)(4,1)S(1)}, pred[6]{0:T(512)(128)(4,1)}, u32[]{:S(2)}) copy-start(pred[6]{0:T(512)(128)(4,1)} %get-tuple-element.88) | copy-start | bytes 22
  100.5 17.3 %copy-start.11 = (pred[6]{0:T(512)(128)(4,1)S(1)}, pred[6]{0:T(512)(128)(4,1)}, u32[]{:S(2)}) copy-start(pred[6]{0:T(512)(128)(4,1)} %get-tuple-element.87) | copy-start | bytes 22
  100.5 17.3 %copy-start.5 = (pred[6]{0:T(512)(128)(4,1)S(1)}, pred[6]{0:T(512)(128)(4,1)}, u32[]{:S(2)}) copy-start(pred[6]{0:T(512)(128)(4,1)} %get-tuple-element.67) | copy-start | bytes 22
  100.5 17.3 %copy-start.6 = (pred[6]{0:T(512)(128)(4,1)S(1)}, pred[6]{0:T(512)(128)(4,1)}, u32[]{:S(2)}) copy-start(pred[6]{0:T(512)(128)(4,1)} %get-tuple-element.82) | copy-start | bytes 22
  100.5 17.3 %copy-start.7 = (pred[6]{0:T(512)(128)(4,1)S(1)}, pred[6]{0:T(512)(128)(4,1)}, u32[]{:S(2)}) copy-start(pred[6]{0:T(512)(128)(4,1)} %get-tuple-element.83) | copy-start | bytes 22
  100.5 17.3 %copy-start.8 = (pred[6]{0:T(512)(128)(4,1)S(1)}, pred[6]{0:T(512)(128)(4,1)}, u32[]{:S(2)}) copy-start(pred[6]{0:T(512)(128)(4,1)} %get-tuple-element.84) | copy-start | bytes 22
  100.5 17.3 %copy-start.9 = (pred[6]{0:T(512)(128)(4,1)S(1)}, pred[6]{0:T(512)(128)(4,1)}, u32[]{:S(2)}) copy-start(pred[6]{0:T(512)(128)(4,1)} %get-tuple-element.85) | copy-start | bytes 22
  100.5 17.3 %copy-start.10 = (pred[6]{0:T(512)(128)(4,1)S(1)}, pred[6]{0:T(512)(128)(4,1)}, u32[]{:S(2)}) copy-start(pred[6]{0:T(512)(128)(4,1)} %get-tuple-element.86) | copy-start | bytes 22
  100.5 17.5 %copy-start.2 = (bf16[256,6,128]{2,0,1:T(8,128)(2,1)S(1)}, bf16[256,6,128]{2,0,1:T(8,128)(2,1)}, u32[]{:S(2)}) copy-start(bf16[256,6,128]{2,0,1:T(8,128)(2,1)} %get-tuple-element.80) | copy-start | bytes 1179652
  101.8 34.4 %copy-start.3 = (pred[6]{0:T(512)(128)(4,1)S(1)}, pred[6]{0:T(512)(128)(4,1)}, u32[]{:S(2)}) copy-start(pred[6]{0:T(512)(128)(4,1)} %get-tuple-element.90) | copy-start | bytes 22
  101.8 34.7 %collective-permute-start.12 = (bf16[256,6,128]{2,0,1:T(8,128)(2,1)}, bf16[256,6,128]{2,0,1:T(8,128)(2,1)S(1)}, u32[]{:S(2)}, u32[]{:S(2)}) collective-permute-start(bf16[256,6,128]{2,0,1:T(8,128)(2,1)} %get-tuple-element.80), channel_id=1, source_target_pairs={{8,0},{12,4},{9,1},{13,5},{10,2},{14,6},{11,3},{15,7},{24,16},{28,... | collective-permute-start | bytes 1179656 | tf_op jit(solution)/shard_map/ppermute | solution.py:14
  103.1 33.3 %collective-permute-start.11 = (bf16[256,6,128]{2,0,1:T(8,128)(2,1)}, bf16[256,6,128]{2,0,1:T(8,128)(2,1)S(1)}, u32[]{:S(2)}, u32[]{:S(2)}) collective-permute-start(bf16[256,6,128]{2,0,1:T(8,128)(2,1)} %get-tuple-element.80), channel_id=1, source_target_pairs={{4,0},{8,4},{12,8},{5,1},{9,5},{13,9},{6,2},{10,6},{14,10},{7,3},{... | collective-permute-start | bytes 1179656 | tf_op jit(solution)/shard_map/ppermute | solution.py:14
  104.4 32.2 %collective-permute-start.13 = (bf16[256,6,128]{2,0,1:T(8,128)(2,1)}, bf16[256,6,128]{2,0,1:T(8,128)(2,1)S(1)}, u32[]{:S(2)}, u32[]{:S(2)}) collective-permute-start(bf16[256,6,128]{2,0,1:T(8,128)(2,1)} %get-tuple-element.80), channel_id=1, source_target_pairs={{12,0},{13,1},{14,2},{15,3},{28,16},{29,17},{30,18},{31,19}} | collective-permute-start | bytes 1179656 | tf_op jit(solution)/shard_map/ppermute | solution.py:14
  105.7 16.1 %collective-permute-start.8 = (bf16[256,6,128]{2,0,1:T(8,128)(2,1)}, bf16[256,6,128]{2,0,1:T(8,128)(2,1)S(1)}, u32[]{:S(2)}, u32[]{:S(2)}) collective-permute-start(bf16[256,6,128]{2,0,1:T(8,128)(2,1)} %get-tuple-element.80), channel_id=1, source_target_pairs={{0,12},{1,13},{2,14},{3,15},{16,28},{17,29},{18,30},{19,31}} | collective-permute-start | bytes 1179656 | tf_op jit(solution)/shard_map/ppermute | solution.py:14
  113.4 4.7 %collective-permute-start.7 = (bf16[256,6,128]{2,0,1:T(8,128)(2,1)}, bf16[256,6,128]{2,0,1:T(8,128)(2,1)S(1)}, u32[]{:S(2)}, u32[]{:S(2)}) collective-permute-start(bf16[256,6,128]{2,0,1:T(8,128)(2,1)} %get-tuple-element.80), channel_id=1, source_target_pairs={} | collective-permute-start | bytes 1179656 | tf_op jit(solution)/shard_map/ppermute | solution.py:14
  118.1 18.0 %collective-permute-start.10 = (bf16[256,6,128]{2,0,1:T(8,128)(2,1)S(1)}, bf16[256,6,128]{2,0,1:T(8,128)(2,1)S(1)}, u32[]{:S(2)}, u32[]{:S(2)}) collective-permute-start(bf16[256,6,128]{2,0,1:T(8,128)(2,1)S(1)} %copy-done.2), channel_id=1, source_target_pairs={{0,4},{4,8},{8,12},{1,5},{5,9},{9,13},{2,6},{6,10},{10,14},{3,7},{... | collective-permute-start | bytes 1179656 | tf_op jit(solution)/shard_map/ppermute | solution.py:14
  121.8 14.1 %collective-permute-start.9 = (bf16[256,6,128]{2,0,1:T(8,128)(2,1)S(1)}, bf16[256,6,128]{2,0,1:T(8,128)(2,1)S(1)}, u32[]{:S(2)}, u32[]{:S(2)}) collective-permute-start(bf16[256,6,128]{2,0,1:T(8,128)(2,1)S(1)} %copy-done.2), channel_id=1, source_target_pairs={{0,8},{4,12},{1,9},{5,13},{2,10},{6,14},{3,11},{7,15},{16,24},{20,... | collective-permute-start | bytes 1179656 | tf_op jit(solution)/shard_map/ppermute | solution.py:14
  139.0 1.3 copy-start.15
  139.0 1.4 copy-start.17
Sparse Core Ops, SparseCore 0:
  9.0 12.5 all-gather.6
  23.1 11.2 all-gather.8
  36.0 10.9 all-gather.4
  140.4 20.2 all-gather.10
where the time goes:
time: 172 us
  waiting for transfers between devices  48 us (28%)
  starting transfers between devices  34.5 us (20%)
  local copies, waits for them, and re-layouts  25.8 us (15%)
  blocking collectives  21 us (12%)
  other arithmetic  18.7 us (11%)
  between operations  13.8 us (8%)
  matrix products  9.75 us (6%)
    ppermute x14, starting transfers between devices, from_behind(): return lax.ppermute(block, axis, route)  34.4 us
    all_gather x1, waiting for transfers between devices, local(): every_result = lax.all_gather(finished, 'head', axis=2, tiled=True)  20 us
    ppermute x14, waiting for transfers between devices, from_behind(): return lax.ppermute(block, axis, route)  15.1 us
    all_gather x1, blocking collectives, spatial(): lax.all_gather(value_rows, 'space', axis=0, tiled=True)  10.8 us
    all_gather x1, blocking collectives, spatial(): lax.all_gather(key_rows, 'space', axis=0, tiled=True)  10.2 us
    all_gather x1, waiting for transfers between devices, local(): lax.all_gather(value_states, 'head', axis=2, tiled=True)  9.68 us
    dot_general x6, matrix products, one_head(): jnp.dot(query_one, key_one.T, preferred_element_type=jnp.float32) * scale  7.5 us
    unnamed x48, local copies, waits for them, and re-layouts  6.23 us
  transfers between devices with their start and end apart: 18, of which 5 were waited for; matrix products, arithmetic and copies ran while one was open for 25% of the time, Pallas kernels for 0%

commit v1 on v0

v1 whole, which is shorter than its diff:
```python
import functools

import jax
import jax.numpy as jnp
from jax import lax
from jax.experimental import pallas as pl
from jax.experimental.pallas import tpu as pltpu
from jax.sharding import PartitionSpec as P

HD = 128
WMAX = 4
MESH = pl.DeviceIdType.MESH


def kernel(
    frames, spaces, cores, prof_ref, win_ref, q_ref, k_ref, v_ref, out_ref,
    full_q, full_k, full_v, kv, tsend, trecv, tout, res, pos, tab,
    loc_sem, d_send, d_recv, s_send, s_recv, t_send, t_recv, o_send, o_recv, r_send, r_recv,
):
    rows = q_ref.shape[1]
    here = q_ref.shape[2] // HD
    heads = here * cores
    share = here // 2
    part = rows // frames
    scale = HD ** (-0.5)
    f = lax.axis_index("frame")
    x = lax.axis_index("space")
    c = lax.axis_index("head")
    others_f = [lax.rem(f + d, frames) for d in range(1, frames)]
    others_x = [lax.rem(x + d, spaces) for d in range(1, spaces)]
    others_c = [lax.rem(c + d, cores) for d in range(1, cores)]
    side = f // (frames // 2)
    far_first = [
        lax.rem(f + (1 - side) * (frames - 1 - i) + side * (1 + i), frames)
        for i in range(frames - 1)
    ]

    def remote(src, dst, send, recv, **target):
        return pltpu.make_async_remote_copy(
            src_ref=src, dst_ref=dst, send_sem=send, recv_sem=recv,
            device_id=target, device_id_type=MESH,
        )

    pairs = ((k_ref, full_k), (v_ref, full_v), (q_ref, full_q))

    def lanes(h):
        return pl.ds(pl.multiple_of(h * HD, HD), HD)

    def own(full):
        return full.at[pl.ds(c * here, here)]

    for n, (src, full) in enumerate(pairs):
        def local_start(h, _):
            pltpu.make_async_copy(
                src.at[0, :, lanes(h)], full.at[c * here + h], loc_sem.at[n]
            ).start()
            return 0

        lax.fori_loop(0, here, local_start, 0)

    barrier = pltpu.get_barrier_semaphore()
    for other in others_c:
        pl.semaphore_signal(barrier, inc=1, device_id={"head": other}, device_id_type=MESH)
    for other in others_x:
        pl.semaphore_signal(barrier, inc=1, device_id={"space": other}, device_id_type=MESH)
    for other in others_f:
        pl.semaphore_signal(barrier, inc=1, device_id={"frame": other}, device_id_type=MESH)
    pl.semaphore_wait(barrier, len(others_c) + len(others_x) + len(others_f))

    for n, (src, full) in enumerate(pairs):
        for other in others_c:
            def core_start(h, _):
                remote(
                    src.at[0, :, lanes(h)], full.at[c * here + h],
                    d_send.at[other, n], d_recv.at[c, n], head=other,
                ).start()
                return 0

            lax.fori_loop(0, here, core_start, 0)

    in_space = jnp.int32(0)
    in_window = jnp.int32(0)
    for h in range(heads):
        p = prof_ref[h]
        rank = p * in_space + (1 - p) * in_window
        core = sum((rank >= share * e).astype(jnp.int32) for e in range(1, cores))
        place = rank + core * (here - share) + (1 - p) * share
        pos[h] = jnp.clip(place, 0, heads - 1)
        in_space = in_space + p
        in_window = in_window + (1 - p)

    def fill(slot, _):
        first = c * here + slot
        second = first + share
        id_s = jnp.int32(0)
        id_w = jnp.int32(0)
        reach = jnp.int32(0)
        for h in range(heads):
            id_s = id_s + jnp.where(pos[h] == first, h, 0)
            is_w = pos[h] == second
            id_w = id_w + jnp.where(is_w, h, 0)
            reach = reach + jnp.where(is_w, win_ref[h], 0)
        tab[0, slot] = jnp.clip(id_s, 0, heads - 1)
        tab[1, slot] = jnp.clip(id_w, 0, heads - 1)
        tab[2, slot] = reach
        return 0

    lax.fori_loop(0, share, fill, 0)

    for n, (src, full) in enumerate(pairs):
        for other in others_c:
            theirs = full.at[pl.ds(other * here, here)]
            remote(theirs, theirs, d_send.at[other, n], d_recv.at[other, n], head=other).wait_recv()
        pltpu.make_async_copy(own(full), own(full), loc_sem.at[n]).wait()

    def pick(full, head):
        return full[head]

    def window_copy(j, other):
        return remote(
            tsend.at[j, other], trecv.at[f, j], t_send.at[other, j], t_recv.at[f, j], frame=other
        )

    def window_gather(j, _):
        head = tab[1, j]
        for n, full in enumerate((full_q, full_k, full_v)):
            block = pick(full, head)
            for g in range(frames):
                tsend[j, g, n] = block[g * part:(g + 1) * part]

        @pl.when(j > 0)
        def _():
            for other in far_first:
                window_copy(j - 1, other).start()

        return 0

    lax.fori_loop(0, share, window_gather, 0)

    my_rows = pl.ds(pl.multiple_of(x * rows, rows), rows)

    def space_copy(j, other):
        return remote(
            kv.at[j, :, my_rows], kv.at[j, :, my_rows], s_send.at[other, j], s_recv.at[x, j], space=other
        )

    def space_gather(j, _):
        head = tab[0, j]
        kv[j, 0, my_rows] = pick(full_k, head)
        kv[j, 1, my_rows] = pick(full_v, head)

        @pl.when(j == 0)
        def _():
            for other in far_first:
                window_copy(share - 1, other).start()

        @pl.when(j > 0)
        def _():
            for other in others_x:
                space_copy(j - 1, other).start()

        return 0

    lax.fori_loop(0, share, space_gather, 0)
    mine = pl.ds(pl.multiple_of(f * part, part), part)

    def out_copy(j, other):
        return remote(
            tout.at[j, other], res.at[c * here + share + j, mine], o_send.at[other, j], o_recv.at[f, j], frame=other
        )

    def back_copy(slot, other):
        return remote(
            res.at[c * here + slot], res.at[c * here + slot], r_send.at[other, slot], r_recv.at[c, slot], head=other
        )

    for other in others_x:
        space_copy(share - 1, other).start()

    def step(j, _):
        for other in others_f:
            remote(
                tsend.at[j, other], trecv.at[other, j], t_send.at[other, j], t_recv.at[other, j], frame=other
            ).wait_recv()
        trecv[f, j] = tsend[j, f]
        reach = tab[2, j]
        qs = [trecv[g, j, 0].astype(jnp.float32) for g in range(frames)]
        ks = [trecv[g, j, 1].astype(jnp.float32) for g in range(frames)]
        vs = [trecv[g, j, 2].astype(jnp.float32) for g in range(frames)]
        for g in range(frames):
            near = [m for m in range(frames) if abs(m - g) <= WMAX]
            scores = []
            for m in near:
                raw = jnp.sum(qs[g] * ks[m], axis=-1, keepdims=True) * scale
                scores.append(jnp.where(reach >= abs(m - g), raw, -1e30))
            peak = functools.reduce(jnp.maximum, scores)
            weights = [jnp.exp(s - peak) for s in scores]
            total = functools.reduce(jnp.add, weights)
            acc = functools.reduce(
                jnp.add,
                [w.astype(jnp.bfloat16).astype(jnp.float32) * vs[m] for w, m in zip(weights, near)],
            )
            tout[j, g] = (acc / total).astype(jnp.bfloat16)
        res[c * here + share + j, mine] = tout[j, f]

        for other in others_x:
            other_rows = pl.ds(pl.multiple_of(other * rows, rows), rows)
            remote(
                kv.at[j, :, other_rows], kv.at[j, :, other_rows],
                s_send.at[other, j], s_recv.at[other, j], space=other,
            ).wait_recv()
        query = pick(full_q, tab[0, j])
        scores = lax.dot_general(
            query, kv[j, 0], (((1,), (1,)), ((), ())), preferred_element_type=jnp.float32
        ) * scale
        peak = jnp.max(scores, axis=1, keepdims=True)
        weights = jnp.exp(scores - peak)
        total = jnp.sum(weights, axis=1, keepdims=True)
        acc = jnp.dot(weights.astype(jnp.bfloat16), kv[j, 1], preferred_element_type=jnp.float32)
        res[c * here + j] = (acc / total).astype(jnp.bfloat16)

        for other in far_first:
            out_copy(j, other).start()

        @pl.when(j > 0)
        def _():
            for other in others_c:
                back_copy(j - 1, other).start()

        return 0

    lax.fori_loop(0, share, step, 0)
    for other in others_c:
        back_copy(share - 1, other).start()

    def forward(j, _):
        for other in others_f:
            theirs = pl.ds(pl.multiple_of(other * part, part), part)
            remote(
                tout.at[j, other], res.at[c * here + share + j, theirs], o_send.at[other, j], o_recv.at[other, j],
                frame=other,
            ).wait_recv()
        for other in others_c:
            back_copy(share + j, other).start()
        return 0

    lax.fori_loop(0, share, forward, 0)

    def arrive(slot, _):
        for other in others_c:
            remote(
                res.at[c * here + slot], res.at[other * here + slot], r_send.at[other, slot], r_recv.at[other, slot], head=other
            ).wait_recv()
        return 0

    lax.fori_loop(0, 2 * share, arrive, 0)

    for i in range(here):
        where = pos[c * here + i]
        out_ref[0, :, i * HD:(i + 1) * HD] = res[where]

    for n, (src, full) in enumerate(pairs):
        for other in others_c:
            remote(own(full), own(full), d_send.at[other, n], d_recv.at[c, n], head=other).wait_send()

    def drain(j, _):
        for other in others_f:
            window_copy(j, other).wait_send()
            out_copy(j, other).wait_send()
        for other in others_x:
            space_copy(j, other).wait_send()
        for other in others_c:
            back_copy(j, other).wait_send()
            back_copy(share + j, other).wait_send()
        return 0

    lax.fori_loop(0, share, drain, 0)


def local(sizes, queries, key_states, value_states, profile, window):
    frames, spaces, cores = sizes
    rows = queries.shape[1]
    here = queries.shape[2] // HD
    share = here // 2
    part = rows // frames
    any_space = pl.BlockSpec(memory_space=pl.ANY)
    smem = pl.BlockSpec(memory_space=pltpu.SMEM)
    bf = jnp.bfloat16
    dma = pltpu.SemaphoreType.DMA
    return pl.pallas_call(
        functools.partial(kernel, frames, spaces, cores),
        out_shape=jax.ShapeDtypeStruct(queries.shape, queries.dtype),
        in_specs=[smem, smem, any_space, any_space, any_space],
        out_specs=pl.BlockSpec(memory_space=pltpu.VMEM),
        scratch_shapes=[
            pltpu.VMEM((cores * here, rows, HD), bf),
            pltpu.VMEM((cores * here, rows, HD), bf),
            pltpu.VMEM((cores * here, rows, HD), bf),
            pltpu.VMEM((share, 2, spaces * rows, HD), bf),
            pltpu.VMEM((share, frames, 3, part, HD), bf),
            pltpu.VMEM((frames, share, 3, part, HD), bf),
            pltpu.VMEM((share, frames, part, HD), bf),
            pltpu.VMEM((cores * 2 * share, rows, HD), bf),
            pltpu.SMEM((here * cores,), jnp.int32),
            pltpu.SMEM((3, share), jnp.int32),
            dma((3,)),
            dma((cores, 3)),
            dma((cores, 3)),
            dma((spaces, share)),
            dma((spaces, share)),
            dma((frames, share)),
            dma((frames, share)),
            dma((frames, share)),
            dma((frames, share)),
            dma((cores, 2 * share)),
            dma((cores, 2 * share)),
        ],
        compiler_params=pltpu.CompilerParams(
            collective_id=0, has_side_effects=True, vmem_limit_bytes=60 * 1024 * 1024
        ),
    )(profile, window, queries, key_states, value_states)


def solution(mesh):
    spec = P(("groups", "frame"), "space", "head")
    sizes = (mesh.shape["frame"], mesh.shape["space"], mesh.shape["head"])
    return jax.shard_map(
        functools.partial(local, sizes),
        mesh=mesh,
        in_specs=(spec, spec, spec, P(), P()),
        out_specs=spec,
        check_vma=False,
    )
```

time: 172 us -> 51.3 us (0.30)
  Pallas kernels: 0 us -> 49.1 us
  waiting for transfers between devices: 48 us -> 0 us
  starting transfers between devices: 34.5 us -> 0 us
  local copies, waits for them, and re-layouts: 25.8 us -> 2.06 us
  blocking collectives: 21 us -> 0 us
  other arithmetic: 18.7 us -> 0 us
  between operations: 13.8 us -> 0.01 us
  matrix products: 9.75 us -> 0 us
    pallas_call x0 -> x1, Pallas kernels: none -> 49.1 us  [local(): pl.pallas_call(functools.partial(kernel, frames, spaces, cores), out_shap...]
    ppermute x14 -> x0, starting transfers between devices: 34.4 us -> none  [from_behind(): return lax.ppermute(block, axis, route)]
    all_gather x4 -> x0, waiting for transfers between devices: 32.8 us -> none  [the longest x1 20 us: local(): every_result = lax.all_gather(finished, 'head', axis=2, tiled=True)]
    all_gather x2 -> x0, blocking collectives: 21 us -> none  [the longest x1 10.8 us: spatial(): lax.all_gather(value_rows, 'space', axis=0, tiled=True)]
    ppermute x14 -> x0, waiting for transfers between devices: 15.1 us -> none  [from_behind(): return lax.ppermute(block, axis, route)]
    dot_general x13 -> x0, matrix products: 9.75 us -> none  [the longest x6 7.5 us: one_head(): jnp.dot(query_one, key_one.T, preferred_element_type=jnp.float32) * scale]
    reshape x6 -> x0, local copies, waits for them, and re-layouts: 7.04 us -> none  [the longest x1 1.91 us: local(): query_all = whole_query.reshape(row_count, H, HD)]
    dynamic_update_slice x18 -> x0, local copies, waits for them, and re-layouts: 4.8 us -> none  [spatial(): lax.map(one_head, (query_major, key_major, value_major) + tuple(start_sta...]
  transfers between devices with their start and end apart: 18 -> 0, of which waited for: 5 -> 0; matrix products, arithmetic and copies ran while one was open for 25% -> 0% of each run, Pallas kernels for 0% -> 0%
where the time goes in v1:
time: 51.3 us; the launch traced here: 51.1 us
  Pallas kernels  49.1 us (96%)
  local copies, waits for them, and re-layouts  2.06 us (4%)
    pallas_call x1, Pallas kernels, local(): pl.pallas_call(functools.partial(kernel, frames, spaces, cores), out_shap...  49.1 us
    unnamed x1, local copies, waits for them, and re-layouts  2.06 us

profile of v1, /device:TPU:0, one launch (start us, length us, event | category | flops | bytes accessed | tf_op | source)
XLA Modules:
  0.0 51.1 jit_solution(9274724816245868337)
XLA Ops:
  0.0 49.1 %shard_map.55 = bf16[1,256,1536]{2,1,0:T(8,128)(2,1)} custom-call(s32[24]{0:T(128)} %prof_ref.1, s32[24]{0:T(128)} %win_ref.1, bf16[1,256,1536]{2,1,0:T(8,128)(2,1)} %q_ref.1, bf16[1,256,1536]{2,1,0:T(8,128)(2,1)} %k_ref.1, bf16[1,256,1536]{2,1,0:T(8,128)(2,1)} %v_ref.1), custom_call_target="tpu_custom_call" | custom-call | tf_op jit(solution)/shard_map/pallas_call | solution.py:290
  49.1 2.1 %copy.7 = bf16[1,256,1536]{2,1,0:T(8,128)(2,1)} copy(bf16[1,256,1536]{2,1,0:T(8,128)(2,1)} %shard_map.55) | data formatting | bytes 1572864

commit v2 on v1

--- a/solution.py
+++ b/solution.py
@@ -9,6 +9,7 @@
 
 HD = 128
 WMAX = 4
+EARLY = 2
 MESH = pl.DeviceIdType.MESH
 
 
@@ -107,53 +108,61 @@
 
     lax.fori_loop(0, share, fill, 0)
 
+    my_rows = pl.ds(pl.multiple_of(x * rows, rows), rows)
+    mine = pl.ds(pl.multiple_of(f * part, part), part)
+
+    def pick(full, head):
+        return full[head]
+
+    def window_copy(j, other):
+        return remote(
+            tsend.at[j, other], trecv.at[f, j], t_send.at[other, j], t_recv.at[f, j], frame=other
+        )
+
+    def window_piece(j, n, other):
+        return remote(
+            tsend.at[j, other, n], trecv.at[f, j, n], t_send.at[other, j], t_recv.at[f, j], frame=other
+        )
+
+    def space_copy(j, other):
+        return remote(
+            kv.at[j, :, my_rows], kv.at[j, :, my_rows], s_send.at[other, j], s_recv.at[x, j], space=other
+        )
+
+    early = min(EARLY, share)
     for n, (src, full) in enumerate(pairs):
         for other in others_c:
             theirs = full.at[pl.ds(other * here, here)]
             remote(theirs, theirs, d_send.at[other, n], d_recv.at[other, n], head=other).wait_recv()
         pltpu.make_async_copy(own(full), own(full), loc_sem.at[n]).wait()
 
-    def pick(full, head):
-        return full[head]
-
-    def window_copy(j, other):
-        return remote(
-            tsend.at[j, other], trecv.at[f, j], t_send.at[other, j], t_recv.at[f, j], frame=other
-        )
-
-    def window_gather(j, _):
-        head = tab[1, j]
-        for n, full in enumerate((full_q, full_k, full_v)):
-            block = pick(full, head)
+        def window_gather(j, _):
+            block = pick(full, tab[1, j])
             for g in range(frames):
                 tsend[j, g, n] = block[g * part:(g + 1) * part]
-
-        @pl.when(j > 0)
-        def _():
+            return 0
+
+        lax.fori_loop(0, share, window_gather, 0)
+
+        def window_early(j, _):
             for other in far_first:
-                window_copy(j - 1, other).start()
-
-        return 0
-
-    lax.fori_loop(0, share, window_gather, 0)
-
-    my_rows = pl.ds(pl.multiple_of(x * rows, rows), rows)
-
-    def space_copy(j, other):
-        return remote(
-            kv.at[j, :, my_rows], kv.at[j, :, my_rows], s_send.at[other, j], s_recv.at[x, j], space=other
-        )
+                window_piece(j, n, other).start()
+            return 0
+
+        lax.fori_loop(0, early, window_early, 0)
+
+    def window_late(j, _):
+        for other in far_first:
+            window_copy(j, other).start()
+        return 0
+
+    lax.fori_loop(early, share, window_late, 0)
 
     def space_gather(j, _):
         head = tab[0, j]
         kv[j, 0, my_rows] = pick(full_k, head)
         kv[j, 1, my_rows] = pick(full_v, head)
 
-        @pl.when(j == 0)
-        def _():
-            for other in far_first:
-                window_copy(share - 1, other).start()
-
         @pl.when(j > 0)
         def _():
             for other in others_x:
@@ -162,7 +171,6 @@
         return 0
 
     lax.fori_loop(0, share, space_gather, 0)
-    mine = pl.ds(pl.multiple_of(f * part, part), part)
 
     def out_copy(j, other):
         return remote(
@@ -184,9 +192,9 @@
             ).wait_recv()
         trecv[f, j] = tsend[j, f]
         reach = tab[2, j]
-        qs = [trecv[g, j, 0].astype(jnp.float32) for g in range(frames)]
-        ks = [trecv[g, j, 1].astype(jnp.float32) for g in range(frames)]
-        vs = [trecv[g, j, 2].astype(jnp.float32) for g in range(frames)]
+        qs = [trecv[g, j, 2].astype(jnp.float32) for g in range(frames)]
+        ks = [trecv[g, j, 0].astype(jnp.float32) for g in range(frames)]
+        vs = [trecv[g, j, 1].astype(jnp.float32) for g in range(frames)]
         for g in range(frames):
             near = [m for m in range(frames) if abs(m - g) <= WMAX]
             scores = []
@@ -289,7 +297,7 @@
     dma = pltpu.SemaphoreType.DMA
     return pl.pallas_call(
         functools.partial(kernel, frames, spaces, cores),
-        out_shape=jax.ShapeDtypeStruct(queries.shape, queries.dtype),
+        out_shape=pltpu.VMEM(queries.shape, queries.dtype),
         in_specs=[smem, smem, any_space, any_space, any_space],
         out_specs=pl.BlockSpec(memory_space=pltpu.VMEM),
         scratch_shapes=[

time: 51.3 us -> 47 us (0.916)
  Pallas kernels: 49.1 us -> 45.9 us
  local copies, waits for them, and re-layouts: 2.06 us -> 0.88 us
    pallas_call x1, Pallas kernels: 49.1 us -> 45.9 us  [local(): pl.pallas_call(functools.partial(kernel, frames, spaces, cores), out_shap...]
    unnamed x1, local copies, waits for them, and re-layouts: 2.06 us -> 0.88 us
where the time goes in v2:
time: 47 us; the launch traced here: 46.8 us
  Pallas kernels  45.9 us (98%)
  local copies, waits for them, and re-layouts  0.88 us (2%)
    pallas_call x1, Pallas kernels, local(): pl.pallas_call(functools.partial(kernel, frames, spaces, cores), out_shap...  45.9 us

profile of v2, /device:TPU:0, one launch (start us, length us, event | category | flops | bytes accessed | tf_op | source)
XLA Modules:
  0.0 46.8 jit_solution(14117626318960907906)
XLA Ops:
  0.0 45.9 %shard_map.55 = bf16[1,256,1536]{2,1,0:T(8,128)(2,1)S(1)} custom-call(s32[24]{0:T(128)} %prof_ref.1, s32[24]{0:T(128)} %win_ref.1, bf16[1,256,1536]{2,1,0:T(8,128)(2,1)} %q_ref.1, bf16[1,256,1536]{2,1,0:T(8,128)(2,1)} %k_ref.1, bf16[1,256,1536]{2,1,0:T(8,128)(2,1)} %v_ref.1), custom_call_target="tpu_custom_call" | custom-call | tf_op jit(solution)/shard_map/pallas_call | solution.py:298
  45.9 0.9 %copy.7 = bf16[1,256,1536]{2,1,0:T(8,128)(2,1)} copy(bf16[1,256,1536]{2,1,0:T(8,128)(2,1)S(1)} %shard_map.55) | data formatting | bytes 1572864

commit v3 on v2

--- a/solution.py
+++ b/solution.py
@@ -9,18 +9,17 @@
 
 HD = 128
 WMAX = 4
-EARLY = 2
 MESH = pl.DeviceIdType.MESH
 
 
 def kernel(
-    frames, spaces, cores, prof_ref, win_ref, q_ref, k_ref, v_ref, out_ref,
-    full_q, full_k, full_v, kv, tsend, trecv, tout, res, pos, tab,
+    frames, spaces, cores, prof_hbm, win_hbm, q_ref, k_ref, v_ref, out_ref,
+    full, mine_first, theirs, squery, kv, tsend, trecv, tout, res,
+    prof_ref, win_ref, pos, place, order, reaches, tab,
     loc_sem, d_send, d_recv, s_send, s_recv, t_send, t_recv, o_send, o_recv, r_send, r_recv,
 ):
     rows = q_ref.shape[1]
     here = q_ref.shape[2] // HD
-    heads = here * cores
     share = here // 2
     part = rows // frames
     scale = HD ** (-0.5)
@@ -42,19 +41,19 @@
             device_id=target, device_id_type=MESH,
         )
 
-    pairs = ((k_ref, full_k), (v_ref, full_v), (q_ref, full_q))
-
     def lanes(h):
         return pl.ds(pl.multiple_of(h * HD, HD), HD)
 
-    def own(full):
-        return full.at[pl.ds(c * here, here)]
-
-    for n, (src, full) in enumerate(pairs):
+    small = (
+        pltpu.make_async_copy(prof_hbm, prof_ref, loc_sem.at[3]),
+        pltpu.make_async_copy(win_hbm, win_ref, loc_sem.at[4]),
+    )
+    for copy in small:
+        copy.start()
+    sources = (k_ref, v_ref, q_ref)
+    for n, src in enumerate(sources):
         def local_start(h, _):
-            pltpu.make_async_copy(
-                src.at[0, :, lanes(h)], full.at[c * here + h], loc_sem.at[n]
-            ).start()
+            pltpu.make_async_copy(src.at[0, :, lanes(h)], full.at[n, h], loc_sem.at[n]).start()
             return 0
 
         lax.fori_loop(0, here, local_start, 0)
@@ -66,102 +65,101 @@
         pl.semaphore_signal(barrier, inc=1, device_id={"space": other}, device_id_type=MESH)
     for other in others_f:
         pl.semaphore_signal(barrier, inc=1, device_id={"frame": other}, device_id_type=MESH)
+
+    for copy in small:
+        copy.wait()
+
+    count = jnp.int32(0)
+    for h in range(here):
+        count = count + prof_ref[h]
+    first_space = (count >= share).astype(jnp.int32)
+    main_count = jnp.maximum(count, here - count)
+    for e in range(cores):
+        main = first_space if e == 0 else 1 - first_space
+        major = jnp.int32(0)
+        minor = main_count
+        for h in range(here):
+            p = prof_ref[e * here + h]
+            is_main = p * main + (1 - p) * (1 - main)
+            slot = jnp.clip(is_main * major + (1 - is_main) * minor, 0, here - 1)
+            major = major + is_main
+            minor = minor + (1 - is_main)
+            away = ((slot >= share) & (slot < main_count)).astype(jnp.int32)
+            owner = away * (1 - e) + (1 - away) * e
+            pos[e * here + h] = slot
+            place[e * here + h] = owner * here + (1 - p) * share + slot - (slot >= share).astype(jnp.int32) * share
+
+    def fill(slot, _):
+        for e in range(cores):
+            head = jnp.int32(0)
+            reach = jnp.int32(0)
+            for h in range(here):
+                hit = pos[e * here + h] == slot
+                head = head + jnp.where(hit, h, 0)
+                reach = reach + jnp.where(hit, win_ref[e * here + h], 0)
+            order[e, slot] = jnp.clip(head, 0, here - 1)
+            reaches[e, slot] = reach
+        return 0
+
+    lax.fori_loop(0, here, fill, 0)
+
+    for n in range(3):
+        pltpu.make_async_copy(full.at[n], full.at[n], loc_sem.at[n]).wait()
+
+    def arrange(slot, _):
+        head = order[c, slot]
+        for n in range(3):
+            mine_first[slot, n] = full[n, head]
+        return 0
+
+    lax.fori_loop(0, here, arrange, 0)
+
     pl.semaphore_wait(barrier, len(others_c) + len(others_x) + len(others_f))
 
-    for n, (src, full) in enumerate(pairs):
-        for other in others_c:
-            def core_start(h, _):
-                remote(
-                    src.at[0, :, lanes(h)], full.at[c * here + h],
-                    d_send.at[other, n], d_recv.at[c, n], head=other,
-                ).start()
-                return 0
-
-            lax.fori_loop(0, here, core_start, 0)
-
-    in_space = jnp.int32(0)
-    in_window = jnp.int32(0)
-    for h in range(heads):
-        p = prof_ref[h]
-        rank = p * in_space + (1 - p) * in_window
-        core = sum((rank >= share * e).astype(jnp.int32) for e in range(1, cores))
-        place = rank + core * (here - share) + (1 - p) * share
-        pos[h] = jnp.clip(place, 0, heads - 1)
-        in_space = in_space + p
-        in_window = in_window + (1 - p)
-
-    def fill(slot, _):
-        first = c * here + slot
-        second = first + share
-        id_s = jnp.int32(0)
-        id_w = jnp.int32(0)
-        reach = jnp.int32(0)
-        for h in range(heads):
-            id_s = id_s + jnp.where(pos[h] == first, h, 0)
-            is_w = pos[h] == second
-            id_w = id_w + jnp.where(is_w, h, 0)
-            reach = reach + jnp.where(is_w, win_ref[h], 0)
-        tab[0, slot] = jnp.clip(id_s, 0, heads - 1)
-        tab[1, slot] = jnp.clip(id_w, 0, heads - 1)
-        tab[2, slot] = reach
-        return 0
-
-    lax.fori_loop(0, share, fill, 0)
-
+    partner = others_c[0]
+
+    def core_copy(j):
+        return remote(mine_first.at[share + j], theirs.at[j], d_send.at[j], d_recv.at[j], head=partner)
+
+    def core_start(j, _):
+        core_copy(j).start()
+        return 0
+
+    lax.fori_loop(0, share, core_start, 0)
+
+    main_space = c * (1 - first_space) + (1 - c) * first_space
     my_rows = pl.ds(pl.multiple_of(x * rows, rows), rows)
     mine = pl.ds(pl.multiple_of(f * part, part), part)
-
-    def pick(full, head):
-        return full[head]
 
     def window_copy(j, other):
         return remote(
             tsend.at[j, other], trecv.at[f, j], t_send.at[other, j], t_recv.at[f, j], frame=other
         )
 
-    def window_piece(j, n, other):
-        return remote(
-            tsend.at[j, other, n], trecv.at[f, j, n], t_send.at[other, j], t_recv.at[f, j], frame=other
-        )
-
     def space_copy(j, other):
         return remote(
             kv.at[j, :, my_rows], kv.at[j, :, my_rows], s_send.at[other, j], s_recv.at[x, j], space=other
         )
 
-    early = min(EARLY, share)
-    for n, (src, full) in enumerate(pairs):
-        for other in others_c:
-            theirs = full.at[pl.ds(other * here, here)]
-            remote(theirs, theirs, d_send.at[other, n], d_recv.at[other, n], head=other).wait_recv()
-        pltpu.make_async_copy(own(full), own(full), loc_sem.at[n]).wait()
-
-        def window_gather(j, _):
-            block = pick(full, tab[1, j])
+    def gather(j, _):
+        core_copy(j).wait_recv()
+        borrowed = share + j < main_count
+        for n in range(3):
+            head_main = mine_first[j, n]
+            head_rest = jnp.where(borrowed, theirs[j, n], mine_first[share + j, n])
+            block = jnp.where(main_space == 1, head_rest, head_main)
             for g in range(frames):
                 tsend[j, g, n] = block[g * part:(g + 1) * part]
-            return 0
-
-        lax.fori_loop(0, share, window_gather, 0)
-
-        def window_early(j, _):
-            for other in far_first:
-                window_piece(j, n, other).start()
-            return 0
-
-        lax.fori_loop(0, early, window_early, 0)
-
-    def window_late(j, _):
+            block = jnp.where(main_space == 1, head_main, head_rest)
+            if n < 2:
+                kv[j, n, my_rows] = block
+            else:
+                squery[j] = block
+        own_reach = reaches[c, j + main_space * share]
+        far_reach = reaches[partner, share + j]
+        tab[j] = jnp.where((main_space == 1) & borrowed, far_reach, own_reach)
         for other in far_first:
             window_copy(j, other).start()
-        return 0
-
-    lax.fori_loop(early, share, window_late, 0)
-
-    def space_gather(j, _):
-        head = tab[0, j]
-        kv[j, 0, my_rows] = pick(full_k, head)
-        kv[j, 1, my_rows] = pick(full_v, head)
 
         @pl.when(j > 0)
         def _():
@@ -170,7 +168,7 @@
 
         return 0
 
-    lax.fori_loop(0, share, space_gather, 0)
+    lax.fori_loop(0, share, gather, 0)
 
     def out_copy(j, other):
         return remote(
@@ -191,7 +189,7 @@
                 tsend.at[j, other], trecv.at[other, j], t_send.at[other, j], t_recv.at[other, j], frame=other
             ).wait_recv()
         trecv[f, j] = tsend[j, f]
-        reach = tab[2, j]
+        reach = tab[j]
         qs = [trecv[g, j, 2].astype(jnp.float32) for g in range(frames)]
         ks = [trecv[g, j, 0].astype(jnp.float32) for g in range(frames)]
         vs = [trecv[g, j, 1].astype(jnp.float32) for g in range(frames)]
@@ -217,7 +215,7 @@
                 kv.at[j, :, other_rows], kv.at[j, :, other_rows],
                 s_send.at[other, j], s_recv.at[other, j], space=other,
             ).wait_recv()
-        query = pick(full_q, tab[0, j])
+        query = squery[j]
         scores = lax.dot_general(
             query, kv[j, 0], (((1,), (1,)), ((), ())), preferred_element_type=jnp.float32
         ) * scale
@@ -264,14 +262,11 @@
     lax.fori_loop(0, 2 * share, arrive, 0)
 
     for i in range(here):
-        where = pos[c * here + i]
-        out_ref[0, :, i * HD:(i + 1) * HD] = res[where]
-
-    for n, (src, full) in enumerate(pairs):
-        for other in others_c:
-            remote(own(full), own(full), d_send.at[other, n], d_recv.at[c, n], head=other).wait_send()
+        out_ref[0, :, i * HD:(i + 1) * HD] = res[place[c * here + i]]
+
 
     def drain(j, _):
+        core_copy(j).wait_send()
         for other in others_f:
             window_copy(j, other).wait_send()
             out_copy(j, other).wait_send()
@@ -292,28 +287,33 @@
     share = here // 2
     part = rows // frames
     any_space = pl.BlockSpec(memory_space=pl.ANY)
-    smem = pl.BlockSpec(memory_space=pltpu.SMEM)
     bf = jnp.bfloat16
     dma = pltpu.SemaphoreType.DMA
     return pl.pallas_call(
         functools.partial(kernel, frames, spaces, cores),
         out_shape=pltpu.VMEM(queries.shape, queries.dtype),
-        in_specs=[smem, smem, any_space, any_space, any_space],
+        in_specs=[any_space] * 5,
         out_specs=pl.BlockSpec(memory_space=pltpu.VMEM),
         scratch_shapes=[
-            pltpu.VMEM((cores * here, rows, HD), bf),
-            pltpu.VMEM((cores * here, rows, HD), bf),
-            pltpu.VMEM((cores * here, rows, HD), bf),
+            pltpu.VMEM((3, here, rows, HD), bf),
+            pltpu.VMEM((here, 3, rows, HD), bf),
+            pltpu.VMEM((share, 3, rows, HD), bf),
+            pltpu.VMEM((share, rows, HD), bf),
             pltpu.VMEM((share, 2, spaces * rows, HD), bf),
             pltpu.VMEM((share, frames, 3, part, HD), bf),
             pltpu.VMEM((frames, share, 3, part, HD), bf),
             pltpu.VMEM((share, frames, part, HD), bf),
             pltpu.VMEM((cores * 2 * share, rows, HD), bf),
             pltpu.SMEM((here * cores,), jnp.int32),
-            pltpu.SMEM((3, share), jnp.int32),
-            dma((3,)),
-            dma((cores, 3)),
-            dma((cores, 3)),
+            pltpu.SMEM((here * cores,), jnp.int32),
+            pltpu.SMEM((here * cores,), jnp.int32),
+            pltpu.SMEM((here * cores,), jnp.int32),
+            pltpu.SMEM((cores, here), jnp.int32),
+            pltpu.SMEM((cores, here), jnp.int32),
+            pltpu.SMEM((share,), jnp.int32),
+            dma((5,)),
+            dma((share,)),
+            dma((share,)),
             dma((spaces, share)),
             dma((spaces, share)),
             dma((frames, share)),

time: 47 us -> 45.8 us (0.974)
  Pallas kernels: 45.9 us -> 44.8 us
    pallas_call x1, Pallas kernels: 45.9 us -> 44.8 us  [local(): pl.pallas_call(functools.partial(kernel, frames, spaces, cores), out_shap...]
where the time goes in v3:
time: 45.8 us; the launch traced here: 45.6 us
  Pallas kernels  44.8 us (98%)
  local copies, waits for them, and re-layouts  0.88 us (2%)
    pallas_call x1, Pallas kernels, local(): pl.pallas_call(functools.partial(kernel, frames, spaces, cores), out_shap...  44.8 us

profile of v3, /device:TPU:0, one launch (start us, length us, event | category | flops | bytes accessed | tf_op | source)
XLA Modules:
  0.0 45.6 jit_solution(5676806663695483886)
XLA Ops:
  0.0 44.8 %shard_map.55 = bf16[1,256,1536]{2,1,0:T(8,128)(2,1)S(1)} custom-call(s32[24]{0:T(128)} %prof_hbm.1, s32[24]{0:T(128)} %win_hbm.1, bf16[1,256,1536]{2,1,0:T(8,128)(2,1)} %q_ref.1, bf16[1,256,1536]{2,1,0:T(8,128)(2,1)} %k_ref.1, bf16[1,256,1536]{2,1,0:T(8,128)(2,1)} %v_ref.1), custom_call_target="tpu_custom_call" | custom-call | tf_op jit(solution)/shard_map/pallas_call | solution.py:292
  44.8 0.9 %copy.7 = bf16[1,256,1536]{2,1,0:T(8,128)(2,1)} copy(bf16[1,256,1536]{2,1,0:T(8,128)(2,1)S(1)} %shard_map.55) | data formatting | bytes 1572864

commit v4 on v3

--- a/solution.py
+++ b/solution.py
@@ -15,7 +15,7 @@
 def kernel(
     frames, spaces, cores, prof_hbm, win_hbm, q_ref, k_ref, v_ref, out_ref,
     full, mine_first, theirs, squery, kv, tsend, trecv, tout, res,
-    prof_ref, win_ref, pos, place, order, reaches, tab,
+    prof_ref, win_ref, pos, place, order, tab,
     loc_sem, d_send, d_recv, s_send, s_recv, t_send, t_recv, o_send, o_recv, r_send, r_recv,
 ):
     rows = q_ref.shape[1]
@@ -90,15 +90,10 @@
             place[e * here + h] = owner * here + (1 - p) * share + slot - (slot >= share).astype(jnp.int32) * share
 
     def fill(slot, _):
-        for e in range(cores):
-            head = jnp.int32(0)
-            reach = jnp.int32(0)
-            for h in range(here):
-                hit = pos[e * here + h] == slot
-                head = head + jnp.where(hit, h, 0)
-                reach = reach + jnp.where(hit, win_ref[e * here + h], 0)
-            order[e, slot] = jnp.clip(head, 0, here - 1)
-            reaches[e, slot] = reach
+        head = jnp.int32(0)
+        for h in range(here):
+            head = head + jnp.where(pos[c * here + h] == slot, h, 0)
+        order[slot] = jnp.clip(head, 0, here - 1)
         return 0
 
     lax.fori_loop(0, here, fill, 0)
@@ -107,7 +102,7 @@
         pltpu.make_async_copy(full.at[n], full.at[n], loc_sem.at[n]).wait()
 
     def arrange(slot, _):
-        head = order[c, slot]
+        head = order[slot]
         for n in range(3):
             mine_first[slot, n] = full[n, head]
         return 0
@@ -155,9 +150,6 @@
                 kv[j, n, my_rows] = block
             else:
                 squery[j] = block
-        own_reach = reaches[c, j + main_space * share]
-        far_reach = reaches[partner, share + j]
-        tab[j] = jnp.where((main_space == 1) & borrowed, far_reach, own_reach)
         for other in far_first:
             window_copy(j, other).start()
 
@@ -169,6 +161,21 @@
         return 0
 
     lax.fori_loop(0, share, gather, 0)
+
+    def fill_reach(j, _):
+        own_slot = j + main_space * share
+        far = ((main_space == 1) & (share + j < main_count)).astype(jnp.int32)
+        own_reach = jnp.int32(0)
+        far_reach = jnp.int32(0)
+        for h in range(here):
+            own_reach = own_reach + jnp.where(pos[c * here + h] == own_slot, win_ref[c * here + h], 0)
+            far_reach = far_reach + jnp.where(
+                pos[partner * here + h] == share + j, win_ref[partner * here + h], 0
+            )
+        tab[j] = far * far_reach + (1 - far) * own_reach
+        return 0
+
+    lax.fori_loop(0, share, fill_reach, 0)
 
     def out_copy(j, other):
         return remote(
@@ -308,8 +315,7 @@
             pltpu.SMEM((here * cores,), jnp.int32),
             pltpu.SMEM((here * cores,), jnp.int32),
             pltpu.SMEM((here * cores,), jnp.int32),
-            pltpu.SMEM((cores, here), jnp.int32),
-            pltpu.SMEM((cores, here), jnp.int32),
+            pltpu.SMEM((here,), jnp.int32),
             pltpu.SMEM((share,), jnp.int32),
             dma((5,)),
             dma((share,)),

time: 45.8 us -> 45.8 us (level)
  no operation moved by 1% of the time
where the time goes in v4:
time: 45.8 us; the launch traced here: 45.6 us
  Pallas kernels  44.7 us (98%)
  local copies, waits for them, and re-layouts  0.88 us (2%)
    pallas_call x1, Pallas kernels, local(): pl.pallas_call(functools.partial(kernel, frames, spaces, cores), out_shap...  44.7 us

profile of v4, /device:TPU:0, one launch (start us, length us, event | category | flops | bytes accessed | tf_op | source)
XLA Modules:
  0.0 45.6 jit_solution(10605894521224390058)
XLA Ops:
  0.0 44.7 %shard_map.55 = bf16[1,256,1536]{2,1,0:T(8,128)(2,1)S(1)} custom-call(s32[24]{0:T(128)} %prof_hbm.1, s32[24]{0:T(128)} %win_hbm.1, bf16[1,256,1536]{2,1,0:T(8,128)(2,1)} %q_ref.1, bf16[1,256,1536]{2,1,0:T(8,128)(2,1)} %k_ref.1, bf16[1,256,1536]{2,1,0:T(8,128)(2,1)} %v_ref.1), custom_call_target="tpu_custom_call" | custom-call | tf_op jit(solution)/shard_map/pallas_call | solution.py:299
  44.7 0.9 %copy.7 = bf16[1,256,1536]{2,1,0:T(8,128)(2,1)} copy(bf16[1,256,1536]{2,1,0:T(8,128)(2,1)S(1)} %shard_map.55) | data formatting | bytes 1572864
